TPU v7x, 128 devices: a whole 4x4x4 slice. The times are simulated.
128 devices in a mesh: row: 16 (over x, z), col: 8 (over y, core).
Axes of the slice: x: 4, y: 4, z: 4, core: 2. Of those that a mesh axis runs over, the one named last changes fastest.
Arguments:
- coarse_kernel: bfloat16 [16, 16, 256, 256], P('col', 'row'), may hold values from -0.03125 to 0.03125
- correlations: bfloat16 [128, 256, 256], P('col'), may hold values from -0.375 to 0.375
- coarse_of: int32 [128], replicated, may hold values from 0 to 15
- energy: float32 [32768], P('row'), may hold values from 1 to 8
- start_vectors: float32 [32768, 64], P(('row', 'col')), may hold values from -6 to 6
Outputs:
- hamiltonian: bfloat16 [32768, 32768], P('row', 'col')
- vectors: float32 [32768, 64], P(('row', 'col'))
- gram: float32 [64, 64], replicated
All inputs are finite; a program needn't handle non-finite values.
Results may differ from a plain program's by a relative error of at most 0.009.
Values may be sent and summed in bfloat16 or wider, within the bound.
A program may use at most 192 MiB of HBM per device.

v0:
```python
import jax
import jax.numpy as jnp
from jax import lax
from jax.sharding import PartitionSpec as P

NK = 128
STEPS = 2


newton_turns = 8


def from_root(x, axis, root):
    return lax.dynamic_index_in_dim(lax.all_gather(x, axis), root, 0, keepdims=False)


def sent_to_all(x, axis):
    devices = lax.axis_size(axis)
    return lax.all_to_all(jnp.broadcast_to(x[None], (devices, *x.shape)), axis, 0, 0, tiled=True)


def laid_out(tiles, dim):
    tiles = jnp.moveaxis(tiles, 0, dim)
    dims = tiles.shape
    return tiles.reshape(*dims[:dim], dims[dim] * dims[dim + 1], *dims[dim + 2 :])


def collect(x, axis, dim):
    tiles = sent_to_all(x, axis)
    return laid_out(tiles, dim)


def in_blocks(x, dim, devices):
    dims = x.shape
    tiles = x.reshape(*dims[:dim], devices, dims[dim] // devices, *dims[dim + 1 :])
    return jnp.moveaxis(tiles, dim, 0)


def edges_of(length, count):
    unit = 8 if length >= 8 * count else 1
    return [length // unit * k // count * unit for k in range(1, count)]


def several_exchanges(x, axis, pieces, split_dim, concat_dim):
    tiles = in_blocks(x, split_dim, lax.axis_size(axis))
    split_at = max(range(1, max(2, tiles.ndim - 1)), key=lambda d: tiles.shape[d])
    outs = []
    for piece in jnp.split(tiles, edges_of(tiles.shape[split_at], pieces), axis=split_at):
        if piece.size:
            outs.append(lax.all_to_all(piece, axis, split_axis=0, concat_axis=0, tiled=True))
    return laid_out(jnp.concatenate(outs, axis=split_at), concat_dim)


def of_everyone(x, axis):
    return sent_to_all(x, axis).sum(axis=0)


def inverse_root(gram):
    size = gram.shape[0]
    identity = jnp.eye(size, dtype=jnp.float32)
    scale_norm = jnp.sqrt(jnp.sum(gram * gram))
    ymat = gram / scale_norm
    zmat = identity
    for turn_index in range(newton_turns):
        middle = 1.5 * identity - 0.5 * jnp.dot(zmat, ymat, precision=lax.Precision.HIGHEST)
        ymat = jnp.dot(ymat, middle, precision=lax.Precision.HIGHEST)
        zmat = jnp.dot(middle, zmat, precision=lax.Precision.HIGHEST)
    return zmat / jnp.sqrt(scale_norm)


def rotate_one(rotation, blocks):
    return jnp.einsum("pa,bpq->baq", rotation, blocks, preferred_element_type=jnp.float32).astype(
        jnp.bfloat16
    )


def per_device(coarse_kernel, correlations, coarse_of, energy, start_vectors):
    rows_total = lax.axis_size("row")
    cols_total = lax.axis_size("col")
    row_index = lax.axis_index("row")
    col_index = lax.axis_index("col")
    fine_rows = NK // rows_total
    fine_cols = correlations.shape[0]
    pair_width = correlations.shape[1]
    offset = row_index * fine_rows % fine_cols
    source = row_index * fine_rows // fine_cols
    own_rows = lax.dynamic_slice_in_dim(correlations, offset, fine_rows, 0)
    left_rot = from_root(own_rows, "col", source)
    strips = collect(coarse_kernel, "col", 0)
    requests = jnp.take(strips, coarse_of, axis=0)
    gathered = several_exchanges(requests, "row", 2, 0, 1)
    col_coarse = lax.dynamic_slice_in_dim(coarse_of, col_index * fine_cols, fine_cols)
    chosen = jnp.take(gathered, col_coarse, axis=1)

    def tile_row(pair):
        rotation, blocks = pair
        blocks = rotate_one(rotation, blocks)
        product = jnp.einsum(
            "kpq,kqs->pks", blocks, correlations, preferred_element_type=jnp.float32
        )
        return product.astype(jnp.bfloat16).reshape(pair_width, fine_cols * pair_width)

    tile_rows = lax.map(tile_row, (left_rot, chosen))
    tile_matrix = tile_rows.reshape(fine_rows * pair_width, fine_cols * pair_width)
    segment = collect(start_vectors.astype(jnp.bfloat16), "col", 0).astype(start_vectors.dtype)
    scale_col = energy[:, None]
    block_rows = segment.shape[0] // cols_total
    gram = jnp.zeros((segment.shape[1], segment.shape[1]), jnp.float32)
    for turn_index in range(STEPS):
        partial_value = lax.dot_general(
            tile_matrix,
            segment.astype(jnp.bfloat16),
            (((0,), (0,)), ((), ())),
            preferred_element_type=jnp.float32,
        )
        summed = lax.psum(partial_value.astype(jnp.bfloat16), "row").astype(jnp.float32)
        own_part = lax.dynamic_slice_in_dim(summed, offset * pair_width, fine_rows * pair_width, 0)
        image = from_root(own_part.astype(jnp.bfloat16), "col", source).astype(own_part.dtype)
        scaled = (image + scale_col * segment) / scale_col
        gram = of_everyone(jnp.dot(scaled.T, scaled, precision=lax.Precision.HIGHEST), "row")
        segment = jnp.dot(scaled, inverse_root(gram), precision=lax.Precision.HIGHEST)
    return (
        tile_matrix,
        lax.dynamic_slice_in_dim(segment, col_index * block_rows, block_rows, 0),
        gram,
    )


def solution(mesh):
    return jax.shard_map(
        per_device,
        mesh=mesh,
        in_specs=(
            P("col", "row", None, None),
            P("col", None, None),
            P(),
            P("row"),
            P(("row", "col"), None),
        ),
        out_specs=(P("row", "col"), P(("row", "col"), None), P()),
        check_vma=False,
    )
```

profile of v0, /device:TPU:0, one launch (start us, length us, event | category | flops | bytes accessed | tf_op | source)
XLA Modules:
  0.0 782.0 jit_solution(5949254283062769564)
XLA Ops:
  9.6 4.6 all-to-all-start
  15.7 25.7 %all-to-all-done = bf16[8,2,1,256,256]{4,3,2,1,0:T(8,128)(2,1)S(1)} async-done(((bf16[8,2,1,256,256]{4,3,2,1,0:T(8,128)(2,1)}), bf16[8,2,1,256,256]{4,3,2,1,0:T(8,128)(2,1)S(1)}, u32[]{:S(2)}, u32[]{:S(2)}) %all-to-all-start) | async-done | bytes 2097184 | tf_op jit(solution)/shard_map/all_to_all | solution.py:19
  41.4 8.4 %gather_fusion = bf16[128,256,256]{2,1,0:T(8,128)(2,1)} fusion(bf16[16,256,256]{2,1,0:T(8,128)(2,1)S(1)} %bitcast.169, s32[1024]{0:T(1024)S(1)} %pad_clamp_fusion.1), kind=kCustom, calls=%fused_computation | custom fusion | bytes 33554944 | tf_op jit(solution)/shard_map/jit(_take)/gather | solution.py:90
  49.8 8.5 %broadcast_select_fusion = bf16[16,8,1,256,256]{4,3,1,0,2:T(8,128)(2,1)S(1)} fusion(bf16[16,8,1,256,256]{4,3,1,0,2:T(8,128)(2,1)} %bitcast.172, pred[16,8]{1,0:T(8,128)(4,1)S(1)} %broadcast_in_dim.62), kind=kLoop, calls=%fused_computation.15 | loop fusion | flops 8388608 | bytes 33554560 | tf_op jit(solution)/shard_map/jit(_take)/select_n | solution.py:90
  58.3 6.4 slice_bitcast_fusion.1
  64.7 8.1 %all-to-all-start.1 = ((bf16[16,8,1,128,256]{4,3,1,2,0:T(8,128)(2,1)}), bf16[16,8,1,128,256]{4,3,1,2,0:T(8,128)(2,1)}, u32[]{:S(2)}, u32[]{:S(2)}) async-start(bf16[16,8,1,128,256]{4,3,1,2,0:T(8,128)(2,1)} %get-tuple-element.68), calls=%async_computation.1 | async-start | bytes 16777216 | tf_op jit(solution)/shard_map/all_to_all | solution.py:50
  73.9 142.8 %all-to-all-done.1 = bf16[16,8,1,128,256]{4,3,1,2,0:T(8,128)(2,1)} async-done(((bf16[16,8,1,128,256]{4,3,1,2,0:T(8,128)(2,1)}), bf16[16,8,1,128,256]{4,3,1,2,0:T(8,128)(2,1)}, u32[]{:S(2)}, u32[]{:S(2)}) %all-to-all-start.1) | async-done | bytes 8388640 | tf_op jit(solution)/shard_map/all_to_all | solution.py:50
  216.8 9.8 %all-to-all-start.2 = ((bf16[16,8,1,128,256]{4,3,1,2,0:T(8,128)(2,1)}), bf16[16,8,1,128,256]{4,3,1,2,0:T(8,128)(2,1)}, u32[]{:S(2)}, u32[]{:S(2)}) async-start(bf16[16,8,1,128,256]{4,3,1,2,0:T(8,128)(2,1)} %get-tuple-element.69), calls=%async_computation.2 | async-start | bytes 16777216 | tf_op jit(solution)/shard_map/all_to_all | solution.py:50
  229.1 116.0 %all-to-all-done.2 = bf16[16,8,1,128,256]{4,3,1,2,0:T(8,128)(2,1)} async-done(((bf16[16,8,1,128,256]{4,3,1,2,0:T(8,128)(2,1)}), bf16[16,8,1,128,256]{4,3,1,2,0:T(8,128)(2,1)}, u32[]{:S(2)}, u32[]{:S(2)}) %all-to-all-start.2) | async-done | bytes 8388640 | tf_op jit(solution)/shard_map/all_to_all | solution.py:50
  345.8 18.7 %all-to-all-start.3 = ((bf16[8,256,64]{1,2,0:T(8,128)(2,1)}), bf16[8,256,64]{1,2,0:T(8,128)(2,1)S(1)}, u32[]{:S(2)}, u32[]{:S(2)}) async-start(bf16[8,256,64]{1,2,0:T(8,128)(2,1)} %broadcast_in_dim.70), calls=%async_computation.3 | async-start | bytes 524288 | tf_op jit(solution)/shard_map/all_to_all | solution.py:19
  364.6 13.8 %copy_bitcast_fusion = bf16[8,16,256,256]{3,2,1,0:T(8,128)(2,1)} fusion(bf16[16,8,1,128,256]{4,3,1,2,0:T(8,128)(2,1)} %all-to-all-done.2, bf16[16,8,1,128,256]{4,3,1,2,0:T(8,128)(2,1)} %all-to-all-done.1), kind=kLoop, calls=%fused_computation.13 | loop fusion | flops 33554432 | bytes 33554432 | tf_op jit(solution)/shard_map/reshape | solution.py:25
  378.4 13.0 %gather_fusion.1 = bf16[16,8,256,256]{3,2,1,0:T(8,128)(2,1)} fusion(bf16[8,16,256,256]{3,2,1,0:T(8,128)(2,1)} %copy_bitcast_fusion, s32[1024]{0:T(1024)S(1)} %pad_clamp_fusion), kind=kCustom, calls=%fused_computation.1 | custom fusion | bytes 33554496 | tf_op jit(solution)/shard_map/jit(_take)/gather | solution.py:93
  391.4 14.2 %select_bitcast_fusion = bf16[8,16,256,256]{3,2,0,1:T(8,128)(2,1)} fusion(bf16[16,8,256,256]{3,2,1,0:T(8,128)(2,1)} %gather_fusion.1, pred[16]{0:T(512)(128)(4,1)S(1)} %get-tuple-element.66), kind=kLoop, calls=%fused_computation.14 | loop fusion | flops 8388608 | bytes 33554448 | tf_op jit(solution)/shard_map/jit(_take)/select_n | solution.py:93
  406.9 45.5 %while.10 = (s32[]{:T(128)}, bf16[8,256,4096]{1,2,0:T(8,128)(2,1)}, bf16[8,16,256,256]{3,2,0,1:T(8,128)(2,1)}, bf16[8,256,256]{2,1,0:T(8,128)(2,1)S(1)}, bf16[16,256,256]{1,2,0:T(8,128)(2,1)}, /*index=5*/s32[]{:T(128)}) while((s32[]{:T(128)}, bf16[8,256,4096]{1,2,0:T(8,128)(2,1)}, bf16[8,16,256,256]{3,2,0,1:T(8,128)(2,1)}, ...), condition=%wide.region_1.2_spmd, body=%wide.region_0.1_spmd.sunk | while | flops 1075838976 | bytes 10618437 | solution.py:103
  407.0 4.2 fusion.185
  412.7 4.2 fusion.185
  418.3 4.2 fusion.185
  424.0 4.2 fusion.185
  429.7 4.2 fusion.185
  435.4 4.2 fusion.185
  441.1 4.2 fusion.185
  446.8 4.2 fusion.185
  452.5 11.7 %fusion.21 = bf16[4096,64]{0,1:T(8,128)(2,1)} fusion(bf16[8,256,4096]{1,2,0:T(8,128)(2,1)} %get-tuple-element.30, bf16[8,256,64]{1,2,0:T(8,128)(2,1)S(1)} %all-to-all-done.3), kind=kOutput, calls=%fused_computation.20 | convolution fusion | flops 1074003968 | bytes 17563648 | tf_op jit(solution)/shard_map/dot_general | solution.py:110
  464.4 90.5 %all-reduce.3.cloned.1.call-done = bf16[4096,64]{0,1:T(8,128)(2,1)} async-done(((bf16[4096,64]{0,1:T(8,128)(2,1)}), bf16[4096,64]{0,1:T(8,128)(2,1)}) %all-reduce.3.cloned.1.call-update) | async-done | bytes 524304 | tf_op jit(solution)/shard_map/psum | solution.py:116
  556.9 25.0 %all-gather.9.cloned.1.call-done = bf16[16384,64]{0,1:T(8,128)(2,1)} async-done(((bf16[2048,64]{0,1:T(8,128)(2,1)}), bf16[16384,64]{0,1:T(8,128)(2,1)}) %all-gather.9.cloned.1.call-update) | async-done | bytes 2097168 | tf_op jit(solution)/shard_map/all_gather | solution.py:14
  587.1 6.9 all-to-all-start.4
  594.2 21.2 %copy.49 = bf16[8,256,4096]{2,1,0:T(8,128)(2,1)} copy(bf16[8,256,4096]{1,2,0:T(8,128)(2,1)} %get-tuple-element.30) | data formatting | bytes 33554432 | tf_op jit(solution)/shard_map/while | solution.py:103
  623.5 9.6 %convolution_convert_fusion = bf16[4096,64]{0,1:T(8,128)(2,1)} fusion(bf16[2048,4096]{1,0:T(8,128)(2,1)} %bitcast.170, f32[2048,64]{0,1:T(8,128)S(1)} %fusion.40), kind=kOutput, calls=%fused_computation.19 | convolution fusion | flops 1074135040 | bytes 17825792 | tf_op jit(solution)/shard_map/dot_general | solution.py:110
  633.4 86.3 %all-reduce.5.cloned.1.call-done = bf16[4096,64]{0,1:T(8,128)(2,1)} async-done(((bf16[4096,64]{0,1:T(8,128)(2,1)}), bf16[4096,64]{0,1:T(8,128)(2,1)}) %all-reduce.5.cloned.1.call-update) | async-done | bytes 524304 | tf_op jit(solution)/shard_map/psum | solution.py:116
  721.4 24.8 %all-gather.11.cloned.1.call-done = bf16[16384,64]{0,1:T(8,128)(2,1)} async-done(((bf16[2048,64]{0,1:T(8,128)(2,1)}), bf16[16384,64]{0,1:T(8,128)(2,1)}) %all-gather.11.cloned.1.call-update) | async-done | bytes 2097168 | tf_op jit(solution)/shard_map/all_gather | solution.py:14
  751.4 6.9 all-to-all-start.5
  758.4 8.9 %all-to-all-done.5 = f32[16,1,4096]{2,1,0:T(1,128)S(1)} async-done(((f32[16,1,4096]{2,1,0:T(1,128)}), f32[16,1,4096]{2,1,0:T(1,128)S(1)}, u32[]{:S(2)}, u32[]{:S(2)}) %all-to-all-start.5) | async-done | bytes 262176 | tf_op jit(solution)/shard_map/all_to_all | solution.py:19
  (118 shorter events, 50.3 us)
Async XLA Ops:
  9.6 31.8 %all-to-all-start = ((bf16[8,2,1,256,256]{4,3,2,1,0:T(8,128)(2,1)}), bf16[8,2,1,256,256]{4,3,2,1,0:T(8,128)(2,1)S(1)}, u32[]{:S(2)}, u32[]{:S(2)}) async-start(bf16[8,2,1,256,256]{4,3,2,1,0:T(8,128)(2,1)} %broadcast_in_dim.65), calls=%async_computation | async-start | bytes 4194304 | tf_op jit(solution)/shard_map/all_to_all | solution.py:19
  64.7 8.2 %copy-start = (bf16[16,256,256]{2,1,0:T(8,128)(2,1)S(1)}, bf16[16,256,256]{2,1,0:T(8,128)(2,1)}, u32[]{:S(2)}) copy-start(bf16[16,256,256]{2,1,0:T(8,128)(2,1)} %param.8) | copy-start | bytes 6291460
  64.7 164.3 %copy-start.2 = (f32[256,64]{0,1:T(8,128)S(1)}, f32[256,64]{0,1:T(8,128)}, u32[]{:S(2)}) copy-start(f32[256,64]{0,1:T(8,128)} %param.11) | copy-start | bytes 196612
  64.7 164.3 %copy-start.3 = (s32[128]{0:T(128)S(1)}, s32[128]{0:T(128)}, u32[]{:S(2)}) copy-start(s32[128]{0:T(128)} %param.9) | copy-start | bytes 1540
  64.7 152.1 %all-to-all-start.1 = ((bf16[16,8,1,128,256]{4,3,1,2,0:T(8,128)(2,1)}), bf16[16,8,1,128,256]{4,3,1,2,0:T(8,128)(2,1)}, u32[]{:S(2)}, u32[]{:S(2)}) async-start(bf16[16,8,1,128,256]{4,3,1,2,0:T(8,128)(2,1)} %get-tuple-element.68), calls=%async_computation.1 | async-start | bytes 16777216 | tf_op jit(solution)/shard_map/all_to_all | solution.py:50
  72.8 332.9 %all-gather.7.cloned.1.call-start = ((), (), s32[]{:S(2)}) async-start(), calls=%async_computation.8 | async-start | bytes 9437184 | tf_op jit(solution)/shard_map/all_gather | solution.py:14
  216.8 128.3 %all-to-all-start.2 = ((bf16[16,8,1,128,256]{4,3,1,2,0:T(8,128)(2,1)}), bf16[16,8,1,128,256]{4,3,1,2,0:T(8,128)(2,1)}, u32[]{:S(2)}, u32[]{:S(2)}) async-start(bf16[16,8,1,128,256]{4,3,1,2,0:T(8,128)(2,1)} %get-tuple-element.69), calls=%async_computation.2 | async-start | bytes 16777216 | tf_op jit(solution)/shard_map/all_to_all | solution.py:50
  345.8 106.6 %all-to-all-start.3 = ((bf16[8,256,64]{1,2,0:T(8,128)(2,1)}), bf16[8,256,64]{1,2,0:T(8,128)(2,1)S(1)}, u32[]{:S(2)}, u32[]{:S(2)}) async-start(bf16[8,256,64]{1,2,0:T(8,128)(2,1)} %broadcast_in_dim.70), calls=%async_computation.3 | async-start | bytes 524288 | tf_op jit(solution)/shard_map/all_to_all | solution.py:19
  364.5 190.4 %all-reduce.3.cloned.1.call-start = ((), (), s32[]{:S(2)}) async-start(), calls=%async_computation.6 | async-start | bytes 1048576 | tf_op jit(solution)/shard_map/psum | solution.py:116
  452.5 132.8 %copy-start.4 = (f32[2048]{0:T(1024)S(1)}, f32[2048]{0:T(1024)}, u32[]{:S(2)}) copy-start(f32[2048]{0:T(1024)} %param.10) | copy-start | bytes 24580
  464.2 117.8 %all-gather.9.cloned.1.call-start = ((), (), s32[]{:S(2)}) async-start(), calls=%async_computation.9 | async-start | bytes 2359296 | tf_op jit(solution)/shard_map/all_gather | solution.py:14
  587.1 28.3 %all-to-all-start.4 = ((f32[16,1,4096]{2,1,0:T(1,128)}), f32[16,1,4096]{2,1,0:T(1,128)S(1)}, u32[]{:S(2)}, u32[]{:S(2)}) async-start(f32[16,1,4096]{2,1,0:T(1,128)} %reshape.136), calls=%async_computation.4 | async-start | bytes 524288 | tf_op jit(solution)/shard_map/all_to_all | solution.py:19
  594.1 125.6 %all-reduce.5.cloned.1.call-start = ((), (), s32[]{:S(2)}) async-start(), calls=%async_computation.7 | async-start | bytes 1048576 | tf_op jit(solution)/shard_map/psum | solution.py:116
  633.1 113.1 %all-gather.11.cloned.1.call-start = ((), (), s32[]{:S(2)}) async-start(), calls=%async_computation.10 | async-start | bytes 2359296 | tf_op jit(solution)/shard_map/all_gather | solution.py:14
  751.4 15.9 %all-to-all-start.5 = ((f32[16,1,4096]{2,1,0:T(1,128)}), f32[16,1,4096]{2,1,0:T(1,128)S(1)}, u32[]{:S(2)}, u32[]{:S(2)}) async-start(f32[16,1,4096]{2,1,0:T(1,128)} %reshape.138), calls=%async_computation.5 | async-start | bytes 524288 | tf_op jit(solution)/shard_map/all_to_all | solution.py:19
  768.8 6.7 copy-start.1
Sparse Core Ops, SparseCore 0:
  75.3 49.2 all-gather.6
  464.3 90.6 all-reduce.2
  557.2 24.6 all-gather.8
  633.3 86.4 all-reduce.4
  721.5 24.6 all-gather.10
where the time goes:
time: 784 us; the launch traced here: 782 us
  waiting for transfers between devices  520 us (66%)
  local copies, waits for them, and re-layouts  79.4 us (10%)
  matrix products  65.5 us (8%)
  starting transfers between devices  55.7 us (7%)
  other arithmetic  45.2 us (6%)
  between operations  15.9 us (2%)
    all_to_all x2, waiting for transfers between devices, several_exchanges(): lax.all_to_all(piece, axis, split_axis=0, concat_axis=0, tiled=True)  259 us
    psum x2, waiting for transfers between devices, per_device(): lax.psum(partial_value.astype(jnp.bfloat16), 'row').astype(jnp.float32)  177 us
    all_gather x3, waiting for transfers between devices, from_root(): lax.all_gather(x, axis)  49.9 us
    all_to_all x4, starting transfers between devices, sent_to_all(): lax.all_to_all(jnp.broadcast_to(x[None], (devices, *x.shape)), axis, 0, 0...  37.2 us
    all_to_all x4, waiting for transfers between devices, sent_to_all(): lax.all_to_all(jnp.broadcast_to(x[None], (devices, *x.shape)), axis, 0, 0...  34.6 us
    dot_general x8, matrix products, tile_row(): jnp.einsum('kpq,kqs->pks', blocks, correlations, preferred_element_type=j...  33.7 us
    while x2, local copies, waits for them, and re-layouts, per_device(): tile_rows = lax.map(tile_row, (left_rot, chosen))  23.6 us
    dot_general x2, matrix products, per_device(): lax.dot_general(tile_matrix, segment.astype(jnp.bfloat16), (((0,), (0,)),...  21.3 us
  transfers between devices with their start and end apart: 11, of which 8 were waited for; matrix products, arithmetic and copies ran while one was open for 15% of the time, Pallas kernels for 0%

commit v1 on v0

v1 whole, which is shorter than its diff:
```python
import functools

import jax
import jax.numpy as jnp
from jax import lax
from jax.experimental import pallas as pl
from jax.experimental.pallas import tpu as pltpu
from jax.sharding import PartitionSpec as P

STEPS = 2
TURNS = 8
F32 = jnp.float32
BF16 = jnp.bfloat16
MESH = pl.DeviceIdType.MESH
ANY = pl.ANY
VMEM = pltpu.VMEM
HIGHEST = lax.Precision.HIGHEST

COLOURS = (
    ((0, 192), "xyz"),
    ((192, 176), "yzx"),
    ((368, 144), "zxy"),
)
N_RING = 6


def place():
    row, col = lax.axis_index("row"), lax.axis_index("col")
    return {
        "x": lax.div(row, 4),
        "z": lax.rem(row, 4),
        "y": lax.div(col, 2),
        "h": lax.rem(col, 2),
    }


def device(at):
    return (at["x"] * 4 + at["z"], at["y"] * 2 + at["h"])


def moved(at, dim, by):
    return {**at, dim: lax.rem(at[dim] + by, 4)}


def gather_kernel(
    unit, corr, start, kall, crow, seg, own_sem, send, recv, dsend, drecv, csend, crecv, ssend, srecv, lsem
):
    me = place()
    row, col = lax.axis_index("row"), lax.axis_index("col")
    partner = {**me, "h": 1 - me["h"]}

    barrier = pltpu.get_barrier_semaphore()
    for dim in "xz":
        for by in (1, 3):
            pl.semaphore_signal(barrier, inc=1, device_id=device(moved(me, dim, by)), device_id_type=MESH)
    for by in range(1, 8):
        pl.semaphore_signal(barrier, inc=1, device_id=(row, lax.rem(col + by, 8)), device_id_type=MESH)
    pl.semaphore_wait(barrier, 11)

    def region(at, whole, rows):
        i = [pl.ds(0, 4) if d in whole else at[d] for d in "yxz"]
        return kall.at[i[0], at["h"], i[1], i[2], pl.ds(*rows), :]

    def halves(rows):
        first, n = rows
        return ((first, n // 2), (first + n // 2, n // 2))

    def copy(src, dst, pair, sems, to):
        return pltpu.make_async_remote_copy(
            src_ref=src,
            dst_ref=dst,
            send_sem=sems[0].at[pair],
            recv_sem=sems[1].at[pair],
            device_id=device(to),
            device_id_type=MESH,
        )

    pending = []

    class Ring:
        def __init__(self, number, dim, rows, whole, at, own=None):
            self.base = number * 6
            self.dim, self.rows, self.whole, self.at, self.own = dim, rows, whole, at, own

        def send(self, slot, at, rows, by, src=None):
            dst = region(at, self.whole, rows)
            c = copy(dst if src is None else src, dst, self.base + slot, (send, recv), moved(me, self.dim, by))
            c.start()
            pending.append(c)

        def got(self, slot, at, rows):
            dst = region(at, self.whole, rows)
            copy(dst, dst, self.base + slot, (send, recv), moved(me, self.dim, 1)).wait_recv()

        def part(self, rows):
            return None if self.own is None else self.own.at[pl.ds(*rows), :]

        def start(self):
            a, b = halves(self.rows)
            self.send(0, self.at, a, 1, self.part(a))
            self.send(1, self.at, b, 3, self.part(b))
            self.send(2, self.at, b, 1, self.part(b))
            self.send(3, self.at, a, 3, self.part(a))

        def forward(self):
            a, b = halves(self.rows)
            self.left, self.right = moved(self.at, self.dim, 3), moved(self.at, self.dim, 1)
            self.got(0, self.left, a)
            self.send(4, self.left, a, 1)
            self.got(1, self.right, b)
            self.send(5, self.right, b, 3)

        def sides(self):
            a, b = halves(self.rows)
            self.got(2, self.left, b)
            self.got(3, self.right, a)
            return (self.left, self.right)

        def far(self):
            a, b = halves(self.rows)
            at = moved(self.at, self.dim, 2)
            self.got(4, at, a)
            self.got(5, at, b)
            return at

    shared = []

    def share(at, whole, rows):
        r = region(at, whole, rows)
        c = copy(r, r, len(shared), (dsend, drecv), partner)
        c.start()
        shared.append((c, {**at, "h": partner["h"]}, whole, rows))

    mine = pltpu.make_async_copy(unit, kall.at[me["y"], me["h"], me["x"], me["z"]], own_sem)
    mine.start()
    rings = [[Ring(c * N_RING, o[0], rows, "", me, unit)] for c, (rows, o) in enumerate(COLOURS)]
    for (first,) in rings:
        first.start()
    unit_there = kall.at[me["y"], me["h"], me["x"], me["z"]]
    to_partner = copy(unit, unit_there, 54, (dsend, drecv), partner)
    to_partner.start()

    def start_copy(by, slot_col, to_col):
        return pltpu.make_async_remote_copy(
            src_ref=start,
            dst_ref=seg.at[slot_col],
            send_sem=ssend.at[by],
            recv_sem=srecv.at[by],
            device_id=(row, to_col),
            device_id_type=MESH,
        )

    seg_mine = pltpu.make_async_copy(start, seg.at[col], lsem.at[0])
    seg_mine.start()
    seg_sent = []
    for by in range(1, 8):
        c = start_copy(by, col, lax.rem(col + by, 8))
        c.start()
        seg_sent.append(c)

    root = lax.div(row, 2)
    offset = lax.rem(row, 2) * 8
    is_root = col == root

    def corr_copy(by, to_col):
        return pltpu.make_async_remote_copy(
            src_ref=corr.at[pl.ds(offset, 8)],
            dst_ref=crow,
            send_sem=csend.at[by],
            recv_sem=crecv,
            device_id=(row, to_col),
            device_id_type=MESH,
        )

    @pl.when(is_root)
    def _():
        c = pltpu.make_async_copy(corr.at[pl.ds(offset, 8)], crow, lsem.at[1])
        c.start()
        for by in range(1, 8):
            corr_copy(by, lax.rem(col + by, 8)).start()

    mine.wait()
    for (first,) in rings:
        first.forward()
    for c, ((rows, o), (first,)) in enumerate(zip(COLOURS, rings)):
        for at in first.sides():
            share(at, "", rows)
        share(first.far(), "", rows)
        second = Ring(c * N_RING + 1, o[1], rows, o[0], me)
        rings[c].append(second)
        second.start()
    for c, (rows, o) in enumerate(COLOURS):
        third = Ring(c * N_RING + 2, o[2], rows, o[0], me)
        rings[c].append(third)
        third.start()
    for r in rings:
        r[1].forward()
    for c, (rows, o) in enumerate(COLOURS):
        for n, at in enumerate(rings[c][1].sides()):
            share(at, o[0], rows)
            ring = Ring(c * N_RING + 3 + n, o[2], rows, o[0], at)
            rings[c].append(ring)
            ring.start()
    for r in rings:
        r[2].forward()
    for c, (rows, o) in enumerate(COLOURS):
        at = rings[c][1].far()
        share(at, o[0], rows)
        ring = Ring(c * N_RING + 5, o[2], rows, o[0], at)
        rings[c].append(ring)
        ring.start()
    for n in (3, 4):
        for r in rings:
            r[n].forward()
    for c, (rows, o) in enumerate(COLOURS):
        for at in rings[c][2].sides():
            share(at, o[0], rows)
        share(rings[c][2].far(), o[0], rows)
    for r in rings:
        r[5].forward()
    for n in (3, 4, 5):
        for c, (rows, o) in enumerate(COLOURS):
            for at in rings[c][n].sides():
                share(at, o[0], rows)
            share(rings[c][n].far(), o[0], rows)

    for c in pending:
        c.wait_send()
    to_partner.wait_send()
    other = kall.at[me["y"], partner["h"], me["x"], me["z"]]
    copy(other, other, 54, (dsend, drecv), partner).wait_recv()
    for n, (c, at, whole, rows) in enumerate(shared):
        c.wait_send()
        r = region(at, whole, rows)
        copy(r, r, n, (dsend, drecv), partner).wait_recv()
    seg_mine.wait()
    for by, c in enumerate(seg_sent, 1):
        c.wait_send()
        start_copy(by, lax.rem(col + 8 - by, 8), col).wait_recv()

    @pl.when(is_root)
    def _():
        pltpu.make_async_copy(corr.at[pl.ds(offset, 8)], crow, lsem.at[1]).wait()
        for by in range(1, 8):
            corr_copy(by, lax.rem(col + by, 8)).wait_send()

    @pl.when(jnp.logical_not(is_root))
    def _():
        corr_copy(1, col).wait_recv()


def gathered(unit, corr, start):
    dma = pltpu.SemaphoreType.DMA
    any_spec = pl.BlockSpec(memory_space=ANY)
    vmem_spec = pl.BlockSpec(memory_space=VMEM)
    return pl.pallas_call(
        gather_kernel,
        out_shape=(
            jax.ShapeDtypeStruct((4, 2, 4, 4, 512, 256), BF16),
            jax.ShapeDtypeStruct((8, 256, 256), BF16),
            jax.ShapeDtypeStruct((8, 64, 256), F32),
        ),
        in_specs=[vmem_spec, any_spec, vmem_spec],
        out_specs=(any_spec, any_spec, any_spec),
        scratch_shapes=[
            dma,
            dma((108,)),
            dma((108,)),
            dma((55,)),
            dma((55,)),
            dma((8,)),
            dma,
            dma((8,)),
            dma((8,)),
            dma((2,)),
        ],
        compiler_params=pltpu.CompilerParams(collective_id=0, has_side_effects=True),
        name="gather",
    )(unit, corr, start)


def tile_kernel(co, pos, *refs):
    blocks, (crow, corr, seg, ham, part, turned, segb) = refs[:8], refs[8:]

    @pl.when(pl.program_id(0) == 0)
    def _():
        for k in range(8):
            turned[k] = crow[k].T
        segb[...] = seg[...].astype(BF16)

    total = jnp.zeros((64, 256), F32)
    for k in range(8):
        left = jnp.dot(turned[k], blocks[k][...], preferred_element_type=F32).astype(BF16)
        tile = jnp.dot(left, corr[...], preferred_element_type=F32).astype(BF16)
        ham[k * 256 : (k + 1) * 256, :] = tile
        total += jnp.dot(segb[k], tile, preferred_element_type=F32)
    part[...] = total.astype(BF16)


def tiled(coarse_of, kall, crow, corr, seg):
    pos = jnp.stack([lax.axis_index("row") * 8, lax.axis_index("col") * 16]).astype(jnp.int32)

    def block(k):
        def index(m, co, pos):
            a, b = co[pos[0] + k], co[pos[1] + m]
            return (a // 4, (a // 2) % 2, b // 4, b % 4, a % 2, 0)

        return pl.BlockSpec((None, None, None, None, 256, 256), index)

    grid_spec = pltpu.PrefetchScalarGridSpec(
        num_scalar_prefetch=2,
        grid=(16,),
        in_specs=[block(k) for k in range(8)]
        + [
            pl.BlockSpec((8, 256, 256), lambda m, co, pos: (0, 0, 0)),
            pl.BlockSpec((None, 256, 256), lambda m, co, pos: (m, 0, 0)),
            pl.BlockSpec((8, 64, 256), lambda m, co, pos: (0, 0, 0)),
        ],
        out_specs=[
            pl.BlockSpec((2048, 256), lambda m, co, pos: (0, m)),
            pl.BlockSpec((None, 64, 256), lambda m, co, pos: (m, 0, 0)),
        ],
        scratch_shapes=[VMEM((8, 256, 256), BF16), VMEM((8, 64, 256), BF16)],
    )
    return pl.pallas_call(
        tile_kernel,
        grid_spec=grid_spec,
        out_shape=(
            jax.ShapeDtypeStruct((2048, 4096), BF16),
            jax.ShapeDtypeStruct((16, 64, 256), BF16),
        ),
        name="tiles",
    )(coarse_of, pos, *([kall] * 8), crow, corr, seg)


def split(x):
    high = x.astype(BF16)
    return high, (x - high.astype(F32)).astype(BF16)


def dot3(rotation, x):
    rh, rl = split(rotation.T)
    xh, xl = split(x)
    lhs = jnp.concatenate([rh, rl, rh], axis=1)
    rhs = jnp.concatenate([xh, xh, xl], axis=0)
    return jnp.dot(lhs, rhs, preferred_element_type=F32)


def inverse_root(gram):
    size = gram.shape[0]
    at = lax.broadcasted_iota(jnp.int32, (size, size), 0)
    identity = jnp.where(at == lax.broadcasted_iota(jnp.int32, (size, size), 1), 1.0, 0.0).astype(F32)
    norm = jnp.sqrt(jnp.sum(gram * gram))
    y = gram / norm
    z = identity
    for _ in range(TURNS):
        t = 1.5 * identity - 0.5 * jnp.dot(z, y, precision=HIGHEST, preferred_element_type=F32)
        y = jnp.dot(y, t, precision=HIGHEST, preferred_element_type=F32)
        z = jnp.dot(t, z, precision=HIGHEST, preferred_element_type=F32)
    return z / jnp.sqrt(norm)


def power_kernel(
    part, ham, energy, seg, vectors, gram_out,
    hamv, parts, image, rsbuf, agbuf, gbuf, gmine, cur, curb,
    hsem, rsend, rrecv, psend, precv, asend, arecv, gsend, grecv,
):
    row, col = lax.axis_index("row"), lax.axis_index("col")
    to_row, to_col = 2 * col + lax.div(row, 8), lax.rem(row, 8)
    own = 8 * row + col
    from_row, from_col = lax.rem(own, 16), lax.div(own, 16)
    moves = jnp.logical_or(to_row != row, to_col != col)

    barrier = pltpu.get_barrier_semaphore()
    for by in range(1, 16):
        pl.semaphore_signal(barrier, inc=1, device_id=(lax.rem(row + by, 16), col), device_id_type=MESH)
    for by in range(1, 8):
        pl.semaphore_signal(barrier, inc=1, device_id=(row, lax.rem(col + by, 8)), device_id_type=MESH)

    @pl.when(moves)
    def _():
        pl.semaphore_signal(barrier, inc=1, device_id=(to_row, to_col), device_id_type=MESH)
        pl.semaphore_signal(barrier, inc=1, device_id=(from_row, from_col), device_id_type=MESH)
        pl.semaphore_wait(barrier, 24)

    @pl.when(jnp.logical_not(moves))
    def _():
        pl.semaphore_wait(barrier, 22)

    fetch = pltpu.make_async_copy(ham, hamv, hsem)
    fetch.start()

    def remote(src, dst, s, r, to):
        return pltpu.make_async_remote_copy(
            src_ref=src, dst_ref=dst, send_sem=s, recv_sem=r, device_id=to, device_id_type=MESH
        )

    cur[...] = seg[...]
    inverse = 1.0 / energy[...]
    for step in range(STEPS):
        last = step == STEPS - 1
        outgoing = part if step == 0 else parts
        sent = []
        for by in range(1, 16):
            to = lax.rem(row + by, 16)
            if step > 0:
                columns = pl.ds(pl.multiple_of(to * 256, 256), 256)
                total = jnp.zeros((64, 256), F32)
                for k in range(8):
                    total += jnp.dot(curb[k], hamv[pl.ds(k * 256, 256), columns], preferred_element_type=F32)
                parts[by] = total.astype(BF16)
                src = parts.at[by]
            else:
                src = part.at[to]
            c = remote(src, rsbuf.at[step, by], rsend.at[step, by], rrecv.at[step, by], (to, col))
            c.start()
            sent.append(c)
        if step > 0:
            columns = pl.ds(pl.multiple_of(row * 256, 256), 256)
            total = jnp.zeros((64, 256), F32)
            for k in range(8):
                total += jnp.dot(curb[k], hamv[pl.ds(k * 256, 256), columns], preferred_element_type=F32)
        else:
            total = part[row].astype(F32)
        for by in range(1, 16):
            remote(
                rsbuf.at[step, by], rsbuf.at[step, by], rsend.at[step, by], rrecv.at[step, by], (row, col)
            ).wait_recv()
            total += rsbuf[step, by].astype(F32)
        image[step] = total.astype(BF16)

        @pl.when(moves)
        def _():
            c = remote(image.at[step], agbuf.at[step, to_col], psend.at[step], precv.at[step], (to_row, to_col))
            c.start()
            c.wait_send()
            remote(
                agbuf.at[step, col], agbuf.at[step, col], psend.at[step], precv.at[step], (row, col)
            ).wait_recv()

        @pl.when(jnp.logical_not(moves))
        def _():
            agbuf[step, col] = image[step]

        for by in range(1, 8):
            to = lax.rem(col + by, 8)
            c = remote(
                agbuf.at[step, col], agbuf.at[step, col], asend.at[step, by], arecv.at[step, by], (row, to)
            )
            c.start()
            sent.append(c)
        for by in range(1, 8):
            slot = lax.rem(col + 8 - by, 8)
            remote(
                agbuf.at[step, slot], agbuf.at[step, slot], asend.at[step, by], arecv.at[step, by], (row, col)
            ).wait_recv()
        square = jnp.zeros((128, 128), F32)
        for k in range(8):
            scaled = agbuf[step, k].astype(F32) * inverse[k : k + 1, :] + cur[k]
            cur[k] = scaled
            both = jnp.concatenate(split(scaled), axis=0)
            square += lax.dot_general(both, both, (((1,), (1,)), ((), ())), preferred_element_type=F32)
        own_gram = (square[:64, :64] + square[64:, 64:]) + (square[:64, 64:] + square[64:, :64])
        packed = jnp.concatenate([own_gram[:32], own_gram[32:]], axis=1)
        gmine[step] = packed
        gbuf[step, row] = packed
        for by in range(1, 16):
            to = lax.rem(row + by, 16)
            c = remote(gmine.at[step], gbuf.at[step, row], gsend.at[step, by], grecv.at[step, by], (to, col))
            c.start()
            sent.append(c)
        for by in range(1, 16):
            slot = lax.rem(row + 16 - by, 16)
            remote(
                gbuf.at[step, slot], gbuf.at[step, slot], gsend.at[step, by], grecv.at[step, by], (row, col)
            ).wait_recv()
        packed = gbuf[step, 0]
        for k in range(1, 16):
            packed += gbuf[step, k]
        gram = jnp.concatenate([packed[:, :64], packed[:, 64:]], axis=0)
        root = inverse_root(gram)
        if last:
            vectors[...] = dot3(root, cur[col])
            gram_out[...] = gram
        else:
            for k in range(8):
                turned = dot3(root, cur[k])
                cur[k] = turned
                curb[k] = turned.astype(BF16)
            fetch.wait()
        for c in sent:
            c.wait_send()


def powered(part, ham, energy, seg):
    dma = pltpu.SemaphoreType.DMA
    any_spec = pl.BlockSpec(memory_space=ANY)
    vmem_spec = pl.BlockSpec(memory_space=VMEM)
    return pl.pallas_call(
        power_kernel,
        out_shape=(jax.ShapeDtypeStruct((64, 256), F32), jax.ShapeDtypeStruct((64, 64), F32)),
        in_specs=[vmem_spec, any_spec, vmem_spec, vmem_spec],
        out_specs=(vmem_spec, vmem_spec),
        scratch_shapes=[
            VMEM((2048, 4096), BF16),
            VMEM((16, 64, 256), BF16),
            VMEM((STEPS, 64, 256), BF16),
            VMEM((STEPS, 16, 64, 256), BF16),
            VMEM((STEPS, 8, 64, 256), BF16),
            VMEM((STEPS, 16, 32, 128), F32),
            VMEM((STEPS, 32, 128), F32),
            VMEM((8, 64, 256), F32),
            VMEM((8, 64, 256), BF16),
            dma,
            dma((STEPS, 16)),
            dma((STEPS, 16)),
            dma((STEPS,)),
            dma((STEPS,)),
            dma((STEPS, 8)),
            dma((STEPS, 8)),
            dma((STEPS, 16)),
            dma((STEPS, 16)),
        ],
        compiler_params=pltpu.CompilerParams(
            collective_id=1, has_side_effects=True, vmem_limit_bytes=48 * 1024 * 1024
        ),
        name="power",
    )(part, ham, energy, seg)


def per_device(coarse_kernel, correlations, coarse_of, energy, start_vectors):
    unit = coarse_kernel.reshape(512, 256)
    kall, crow, seg = gathered(unit, correlations, start_vectors.T)
    ham, part = tiled(coarse_of, kall, crow, correlations, seg)
    vectors, gram = powered(part, ham, energy.reshape(8, 256), seg)
    return ham, vectors.T, gram


def solution(mesh):
    return jax.shard_map(
        per_device,
        mesh=mesh,
        in_specs=(
            P("col", "row", None, None),
            P("col", None, None),
            P(),
            P("row"),
            P(("row", "col"), None),
        ),
        out_specs=(P("row", "col"), P(("row", "col"), None), P()),
        check_vma=False,
    )
```

time: 784 us -> 259 us (0.33)
  waiting for transfers between devices: 520 us -> 0 us
  Pallas kernels: 0 us -> 254 us
  local copies, waits for them, and re-layouts: 79.4 us -> 2.29 us
  matrix products: 65.5 us -> 0 us
  starting transfers between devices: 55.7 us -> 0 us
  other arithmetic: 45.2 us -> 0.64 us
  between operations: 15.9 us -> 0.69 us
    all_to_all x6 -> x0, waiting for transfers between devices: 293 us -> none  [the longest x2 259 us: several_exchanges(): lax.all_to_all(piece, axis, split_axis=0, concat_axis=0, tiled=True)]
    pallas_call x0 -> x3, Pallas kernels: none -> 254 us  [the longest x1 140 us: gathered(): pl.pallas_call(gather_kernel, out_shape=(jax.ShapeDtypeStruct((4, 2, 4, 4...]
    psum x2 -> x0, waiting for transfers between devices: 177 us -> none  [per_device(): lax.psum(partial_value.astype(jnp.bfloat16), 'row').astype(jnp.float32)]
    dot_general x60 -> x0, matrix products: 65.5 us -> none  [the longest x8 33.7 us: tile_row(): jnp.einsum('kpq,kqs->pks', blocks, correlations, preferred_element_type=j...]
    all_to_all x6 -> x0, starting transfers between devices: 55.1 us -> none  [the longest x4 37.2 us: sent_to_all(): lax.all_to_all(jnp.broadcast_to(x[None], (devices, *x.shape)), axis, 0, 0...]
    all_gather x3 -> x0, waiting for transfers between devices: 49.9 us -> none  [from_root(): lax.all_gather(x, axis)]
    while x2 -> x0, local copies, waits for them, and re-layouts: 23.6 us -> none  [per_device(): tile_rows = lax.map(tile_row, (left_rot, chosen))]
    select_n x3 -> x0, other arithmetic: 23.4 us -> none  [the longest x1 14.2 us: per_device(): chosen = jnp.take(gathered, col_coarse, axis=1)]
  transfers between devices with their start and end apart: 11 -> 0, of which waited for: 8 -> 0; matrix products, arithmetic and copies ran while one was open for 15% -> 0% of each run, Pallas kernels for 0% -> 0%
where the time goes in v1:
time: 259 us; the launch traced here: 258 us
  Pallas kernels  254 us (98%)
    pallas_call x1, Pallas kernels, gathered(): pl.pallas_call(gather_kernel, out_shape=(jax.ShapeDtypeStruct((4, 2, 4, 4...  140 us
    pallas_call x1, Pallas kernels, powered(): pl.pallas_call(power_kernel, out_shape=(jax.ShapeDtypeStruct((64, 256), F...  74.4 us
    pallas_call x1, Pallas kernels, tiled(): pl.pallas_call(tile_kernel, grid_spec=grid_spec, out_shape=(jax.ShapeDtyp...  40.4 us

profile of v1, /device:TPU:0, one launch (start us, length us, event | category | flops | bytes accessed | tf_op | source)
XLA Modules:
  0.0 258.0 jit_solution(5488748830944208165)
XLA Ops:
  0.6 139.6 %gather.1 = (bf16[4,2,4,4,512,256]{5,4,3,2,1,0:T(8,128)(2,1)}, bf16[8,256,256]{2,1,0:T(8,128)(2,1)}, f32[8,64,256]{2,1,0:T(8,128)}) custom-call(bf16[512,256]{1,0:T(8,128)(2,1)} %bitcast.6, bf16[16,256,256]{2,1,0:T(8,128)(2,1)} %refs_9_.1, f32[64,256]{1,0:T(8,128)} %bitcast.7), custom_call_target="tpu_custom_call" | custom-call | tf_op jit(solution)/shard_map/gather/pallas_call | solution.py:256
  140.2 0.6 pad_add_fusion.pos
  140.9 0.0 copy-start.2
  140.9 0.0 copy-start
  140.9 40.4 %tiles.1 = (bf16[2048,4096]{1,0:T(8,128)(2,1)}, bf16[16,64,256]{2,1,0:T(8,128)(2,1)}) custom-call(s32[128]{0:T(128)} %co.1, s32[2]{0:T(128)} %pad_add_fusion.pos, bf16[4,2,4,4,512,256]{5,4,3,2,1,0:T(8,128)(2,1)} %get-tuple-element.10.refs_0_.refs_1_.refs_2_.refs_3_.refs_4_.refs_5_.refs_6_.refs_7_, ...), custom_call_target="tpu_custom_call" | custom-call | tf_op jit(solution)/shard_map/tiles/pallas_call | solution.py:325
  181.2 0.0 copy-done.2
  181.2 0.0 copy-done
  181.2 0.0 copy-start.1
  181.3 1.0 copy-done.1
  182.3 74.4 %power.1 = (f32[64,256]{1,0:T(8,128)S(1)}, f32[64,64]{1,0:T(8,128)S(1)}) custom-call(bf16[16,64,256]{2,1,0:T(8,128)(2,1)S(1)} %copy-done.1, bf16[2048,4096]{1,0:T(8,128)(2,1)} %get-tuple-element.20.ham, f32[8,256]{1,0:T(8,128)S(1)} %reshape.13.energy, f32[8,64,256]{2,1,0:T(8,128)S(1)} %copy-done), custom_call_target="tpu_custom_call" | custom-call | tf_op jit(solution)/shard_map/power/pallas_call | solution.py:499
  256.7 0.6 copy.10
  257.3 0.6 copy.11
  (1 shorter events, 0.0 us)
Async XLA Ops:
  140.9 40.4 %copy-start.2 = (f32[2048]{0:T(1024)S(1)}, f32[2048]{0:T(1024)}, u32[]{:S(2)}) copy-start(f32[2048]{0:T(1024)} %param.8) | copy-start | bytes 24580
  140.9 40.4 %copy-start = (f32[8,64,256]{2,1,0:T(8,128)S(1)}, f32[8,64,256]{2,1,0:T(8,128)}, u32[]{:S(2)}) copy-start(f32[8,64,256]{2,1,0:T(8,128)} %get-tuple-element.12.refs_10_.seg) | copy-start | bytes 1572868
  181.2 1.0 copy-start.1

commit v2 on v1

--- a/solution.py
+++ b/solution.py
@@ -158,26 +158,81 @@
         c.start()
         seg_sent.append(c)
 
-    root = lax.div(row, 2)
     offset = lax.rem(row, 2) * 8
-    is_root = col == root
-
-    def corr_copy(by, to_col):
+    away = lax.rem(me["y"] + 4 - me["x"], 4)
+    on_line = me["h"] == lax.div(me["z"], 2)
+
+    def corr_copy(n, first, to, src=crow):
         return pltpu.make_async_remote_copy(
-            src_ref=corr.at[pl.ds(offset, 8)],
-            dst_ref=crow,
-            send_sem=csend.at[by],
-            recv_sem=crecv,
-            device_id=(row, to_col),
+            src_ref=src.at[pl.ds(first, 4)] if src is crow else src.at[pl.ds(offset + first, 4)],
+            dst_ref=crow.at[pl.ds(first, 4)],
+            send_sem=csend.at[n],
+            recv_sem=crecv.at[n],
+            device_id=device(to),
             device_id_type=MESH,
         )
 
-    @pl.when(is_root)
-    def _():
-        c = pltpu.make_async_copy(corr.at[pl.ds(offset, 8)], crow, lsem.at[1])
-        c.start()
-        for by in range(1, 8):
-            corr_copy(by, lax.rem(col + by, 8)).start()
+    up, down = moved(me, "y", 1), moved(me, "y", 3)
+
+    def corr_start():
+        @pl.when(jnp.logical_and(on_line, away == 0))
+        def _():
+            pltpu.make_async_copy(corr.at[pl.ds(offset, 8)], crow, lsem.at[1]).start()
+            corr_copy(0, 0, up, corr).start()
+            corr_copy(1, 4, down, corr).start()
+            corr_copy(2, 4, up, corr).start()
+            corr_copy(3, 0, down, corr).start()
+            corr_copy(4, 0, partner, corr).start()
+            corr_copy(5, 4, partner, corr).start()
+
+    def corr_forward():
+        @pl.when(jnp.logical_and(on_line, away == 1))
+        def _():
+            corr_copy(0, 0, up).wait_recv()
+            corr_copy(0, 0, up).start()
+            corr_copy(4, 0, partner).start()
+            corr_copy(2, 4, up).wait_recv()
+            corr_copy(5, 4, partner).start()
+
+        @pl.when(jnp.logical_and(on_line, away == 3))
+        def _():
+            corr_copy(1, 4, down).wait_recv()
+            corr_copy(1, 4, down).start()
+            corr_copy(5, 4, partner).start()
+            corr_copy(3, 0, down).wait_recv()
+            corr_copy(4, 0, partner).start()
+
+    def corr_finish():
+        @pl.when(jnp.logical_and(on_line, away == 0))
+        def _():
+            pltpu.make_async_copy(corr.at[pl.ds(offset, 8)], crow, lsem.at[1]).wait()
+            for n, first in enumerate((0, 4, 4, 0)):
+                corr_copy(n, first, up).wait_send()
+
+        @pl.when(jnp.logical_and(on_line, away == 1))
+        def _():
+            corr_copy(0, 0, up).wait_send()
+
+        @pl.when(jnp.logical_and(on_line, away == 3))
+        def _():
+            corr_copy(1, 4, up).wait_send()
+
+        @pl.when(jnp.logical_and(on_line, away == 2))
+        def _():
+            corr_copy(0, 0, up).wait_recv()
+            corr_copy(4, 0, partner).start()
+            corr_copy(1, 4, down).wait_recv()
+            corr_copy(5, 4, partner).start()
+
+        @pl.when(on_line)
+        def _():
+            corr_copy(4, 0, partner).wait_send()
+            corr_copy(5, 4, partner).wait_send()
+
+        @pl.when(jnp.logical_not(on_line))
+        def _():
+            corr_copy(4, 0, partner).wait_recv()
+            corr_copy(5, 4, partner).wait_recv()
 
     mine.wait()
     for (first,) in rings:
@@ -193,6 +248,7 @@
         third = Ring(c * N_RING + 2, o[2], rows, o[0], me)
         rings[c].append(third)
         third.start()
+    corr_start()
     for r in rings:
         r[1].forward()
     for c, (rows, o) in enumerate(COLOURS):
@@ -212,6 +268,7 @@
     for n in (3, 4):
         for r in rings:
             r[n].forward()
+    corr_forward()
     for c, (rows, o) in enumerate(COLOURS):
         for at in rings[c][2].sides():
             share(at, o[0], rows)
@@ -238,15 +295,7 @@
         c.wait_send()
         start_copy(by, lax.rem(col + 8 - by, 8), col).wait_recv()
 
-    @pl.when(is_root)
-    def _():
-        pltpu.make_async_copy(corr.at[pl.ds(offset, 8)], crow, lsem.at[1]).wait()
-        for by in range(1, 8):
-            corr_copy(by, lax.rem(col + by, 8)).wait_send()
-
-    @pl.when(jnp.logical_not(is_root))
-    def _():
-        corr_copy(1, col).wait_recv()
+    corr_finish()
 
 
 def gathered(unit, corr, start):
@@ -268,8 +317,8 @@
             dma((108,)),
             dma((55,)),
             dma((55,)),
-            dma((8,)),
-            dma,
+            dma((6,)),
+            dma((6,)),
             dma((8,)),
             dma((8,)),
             dma((2,)),
@@ -280,32 +329,33 @@
 
 
 def tile_kernel(co, pos, *refs):
-    blocks, (crow, corr, seg, ham, part, turned, segb) = refs[:8], refs[8:]
+    blocks, (crow, corr, seg, ham, part, turned, segb, lefts) = refs[:8], refs[8:]
 
     @pl.when(pl.program_id(0) == 0)
     def _():
         for k in range(8):
             turned[k] = crow[k].T
-        segb[...] = seg[...].astype(BF16)
-
-    total = jnp.zeros((64, 256), F32)
+            segb[:, k * 256 : (k + 1) * 256] = seg[k].astype(BF16)
+
     for k in range(8):
-        left = jnp.dot(turned[k], blocks[k][...], preferred_element_type=F32).astype(BF16)
-        tile = jnp.dot(left, corr[...], preferred_element_type=F32).astype(BF16)
-        ham[k * 256 : (k + 1) * 256, :] = tile
-        total += jnp.dot(segb[k], tile, preferred_element_type=F32)
-    part[...] = total.astype(BF16)
+        left = jnp.dot(turned[k], blocks[k][...], preferred_element_type=F32)
+        lefts[k * 256 : (k + 1) * 256, :] = left.astype(BF16)
+    tile = jnp.dot(lefts[...], corr[...], preferred_element_type=F32).astype(BF16)
+    ham[...] = tile
+    part[...] = jnp.dot(segb[...], tile, preferred_element_type=F32).astype(BF16)
 
 
 def tiled(coarse_of, kall, crow, corr, seg):
     pos = jnp.stack([lax.axis_index("row") * 8, lax.axis_index("col") * 16]).astype(jnp.int32)
+
+    kall = kall.reshape(8, 16, 2, 256, 256)
 
     def block(k):
         def index(m, co, pos):
             a, b = co[pos[0] + k], co[pos[1] + m]
-            return (a // 4, (a // 2) % 2, b // 4, b % 4, a % 2, 0)
-
-        return pl.BlockSpec((None, None, None, None, 256, 256), index)
+            return (lax.div(a, 2), b, lax.rem(a, 2), 0, 0)
+
+        return pl.BlockSpec((None, None, None, 256, 256), index)
 
     grid_spec = pltpu.PrefetchScalarGridSpec(
         num_scalar_prefetch=2,
@@ -320,7 +370,7 @@
             pl.BlockSpec((2048, 256), lambda m, co, pos: (0, m)),
             pl.BlockSpec((None, 64, 256), lambda m, co, pos: (m, 0, 0)),
         ],
-        scratch_shapes=[VMEM((8, 256, 256), BF16), VMEM((8, 64, 256), BF16)],
+        scratch_shapes=[VMEM((8, 256, 256), BF16), VMEM((64, 2048), BF16), VMEM((2048, 256), BF16)],
     )
     return pl.pallas_call(
         tile_kernel,

time: 259 us -> 190 us (0.73)
  Pallas kernels: 254 us -> 185 us
    pallas_call x1, Pallas kernels: 140 us -> 93.1 us  [gathered(): pl.pallas_call(gather_kernel, out_shape=(jax.ShapeDtypeStruct((4, 2, 4, 4...]
    pallas_call x1, Pallas kernels: 40.4 us -> 25 us  [tiled(): pl.pallas_call(tile_kernel, grid_spec=grid_spec, out_shape=(jax.ShapeDtyp...]
    pallas_call x1, Pallas kernels: 74.4 us -> 67.2 us  [powered(): pl.pallas_call(power_kernel, out_shape=(jax.ShapeDtypeStruct((64, 256), F...]
where the time goes in v2:
time: 190 us; the launch traced here: 189 us
  Pallas kernels  185 us (97%)
  local copies, waits for them, and re-layouts  2.29 us (1%)
    pallas_call x1, Pallas kernels, gathered(): pl.pallas_call(gather_kernel, out_shape=(jax.ShapeDtypeStruct((4, 2, 4, 4...  93.1 us
    pallas_call x1, Pallas kernels, powered(): pl.pallas_call(power_kernel, out_shape=(jax.ShapeDtypeStruct((64, 256), F...  67.2 us
    pallas_call x1, Pallas kernels, tiled(): pl.pallas_call(tile_kernel, grid_spec=grid_spec, out_shape=(jax.ShapeDtyp...  25 us

profile of v2, /device:TPU:0, one launch (start us, length us, event | category | flops | bytes accessed | tf_op | source)
XLA Modules:
  0.0 189.0 jit_solution(325776651757529741)
XLA Ops:
  0.6 93.1 %gather.1 = (bf16[4,2,4,4,512,256]{5,4,3,2,1,0:T(8,128)(2,1)}, bf16[8,256,256]{2,1,0:T(8,128)(2,1)}, f32[8,64,256]{2,1,0:T(8,128)}) custom-call(bf16[512,256]{1,0:T(8,128)(2,1)} %bitcast.15, bf16[16,256,256]{2,1,0:T(8,128)(2,1)} %refs_9_.1, f32[64,256]{1,0:T(8,128)} %bitcast.16), custom_call_target="tpu_custom_call" | custom-call | tf_op jit(solution)/shard_map/gather/pallas_call | solution.py:305
  93.8 0.6 pad_add_fusion.pos
  94.4 0.0 copy-start.2
  94.4 0.0 copy-start
  94.4 25.0 %tiles.1 = (bf16[2048,4096]{1,0:T(8,128)(2,1)}, bf16[16,64,256]{2,1,0:T(8,128)(2,1)}) custom-call(s32[128]{0:T(128)} %co.1, s32[2]{0:T(128)} %pad_add_fusion.pos, bf16[8,16,2,256,256]{4,3,2,1,0:T(8,128)(2,1)} %bitcast.7, bf16[8,16,2,256,256]{4,3,2,1,0:T(8,128)(2,1)} %bitcast.8, bf16[8,16,2,256,256]{4,3,2,1,0:T(8,128)(2,1)} %bitcast.9, ...), custom_call_target="tpu_custom_call" | custom-call | tf_op jit(solution)/shard_map/tiles/pallas_call | solution.py:375
  119.4 0.0 copy-done.2
  119.4 0.0 copy-done
  119.4 0.0 copy-start.1
  119.4 1.0 copy-done.1
  120.5 67.2 %power.1 = (f32[64,256]{1,0:T(8,128)S(1)}, f32[64,64]{1,0:T(8,128)S(1)}) custom-call(bf16[16,64,256]{2,1,0:T(8,128)(2,1)S(1)} %copy-done.1, bf16[2048,4096]{1,0:T(8,128)(2,1)} %get-tuple-element.20.ham, f32[8,256]{1,0:T(8,128)S(1)} %reshape.17.energy, f32[8,64,256]{2,1,0:T(8,128)S(1)} %copy-done), custom_call_target="tpu_custom_call" | custom-call | tf_op jit(solution)/shard_map/power/pallas_call | solution.py:549
  187.7 0.6 copy.10
  188.4 0.6 copy.11
  (1 shorter events, 0.0 us)
Async XLA Ops:
  94.4 25.0 %copy-start.2 = (f32[2048]{0:T(1024)S(1)}, f32[2048]{0:T(1024)}, u32[]{:S(2)}) copy-start(f32[2048]{0:T(1024)} %param.8) | copy-start | bytes 24580
  94.4 25.0 %copy-start = (f32[8,64,256]{2,1,0:T(8,128)S(1)}, f32[8,64,256]{2,1,0:T(8,128)}, u32[]{:S(2)}) copy-start(f32[8,64,256]{2,1,0:T(8,128)} %get-tuple-element.12.refs_10_.seg) | copy-start | bytes 1572868
  119.4 1.0 copy-start.1

commit v3 on v2

--- a/solution.py
+++ b/solution.py
@@ -51,11 +51,11 @@
 
     barrier = pltpu.get_barrier_semaphore()
     for dim in "xz":
-        for by in (1, 3):
+        for by in (1, 2, 3):
             pl.semaphore_signal(barrier, inc=1, device_id=device(moved(me, dim, by)), device_id_type=MESH)
     for by in range(1, 8):
         pl.semaphore_signal(barrier, inc=1, device_id=(row, lax.rem(col + by, 8)), device_id_type=MESH)
-    pl.semaphore_wait(barrier, 11)
+    pl.semaphore_wait(barrier, 13)
 
     def region(at, whole, rows):
         i = [pl.ds(0, 4) if d in whole else at[d] for d in "yxz"]
@@ -80,6 +80,7 @@
     class Ring:
         def __init__(self, number, dim, rows, whole, at, own=None):
             self.base = number * 6
+            self.direct = own is not None
             self.dim, self.rows, self.whole, self.at, self.own = dim, rows, whole, at, own
 
         def send(self, slot, at, rows, by, src=None):
@@ -97,30 +98,54 @@
 
         def start(self):
             a, b = halves(self.rows)
+            if self.direct:
+                self.send(0, self.at, self.rows, 2, self.part(self.rows))
+                self.send(1, self.at, self.rows, 1, self.part(self.rows))
+                self.send(2, self.at, self.rows, 3, self.part(self.rows))
+                return
             self.send(0, self.at, a, 1, self.part(a))
             self.send(1, self.at, b, 3, self.part(b))
             self.send(2, self.at, b, 1, self.part(b))
             self.send(3, self.at, a, 3, self.part(a))
 
         def forward(self):
+            if self.direct:
+                self.left, self.right = moved(self.at, self.dim, 3), moved(self.at, self.dim, 1)
+                self.got(1, self.left, self.rows)
+                share(self.left, self.whole, self.rows)
+                self.got(2, self.right, self.rows)
+                share(self.right, self.whole, self.rows)
+                return
             a, b = halves(self.rows)
             self.left, self.right = moved(self.at, self.dim, 3), moved(self.at, self.dim, 1)
             self.got(0, self.left, a)
             self.send(4, self.left, a, 1)
+            share(self.left, self.whole, a)
             self.got(1, self.right, b)
             self.send(5, self.right, b, 3)
+            share(self.right, self.whole, b)
 
         def sides(self):
+            if self.direct:
+                return (self.left, self.right)
             a, b = halves(self.rows)
             self.got(2, self.left, b)
+            share(self.left, self.whole, b)
             self.got(3, self.right, a)
+            share(self.right, self.whole, a)
             return (self.left, self.right)
 
         def far(self):
             a, b = halves(self.rows)
             at = moved(self.at, self.dim, 2)
+            if self.direct:
+                self.got(0, at, self.rows)
+                share(at, self.whole, self.rows)
+                return at
             self.got(4, at, a)
+            share(at, self.whole, a)
             self.got(5, at, b)
+            share(at, self.whole, b)
             return at
 
     shared = []
@@ -137,7 +162,7 @@
     for (first,) in rings:
         first.start()
     unit_there = kall.at[me["y"], me["h"], me["x"], me["z"]]
-    to_partner = copy(unit, unit_there, 54, (dsend, drecv), partner)
+    to_partner = copy(unit, unit_there, 108, (dsend, drecv), partner)
     to_partner.start()
 
     def start_copy(by, slot_col, to_col):
@@ -238,9 +263,8 @@
     for (first,) in rings:
         first.forward()
     for c, ((rows, o), (first,)) in enumerate(zip(COLOURS, rings)):
-        for at in first.sides():
-            share(at, "", rows)
-        share(first.far(), "", rows)
+        first.sides()
+        first.far()
         second = Ring(c * N_RING + 1, o[1], rows, o[0], me)
         rings[c].append(second)
         second.start()
@@ -253,39 +277,39 @@
         r[1].forward()
     for c, (rows, o) in enumerate(COLOURS):
         for n, at in enumerate(rings[c][1].sides()):
-            share(at, o[0], rows)
             ring = Ring(c * N_RING + 3 + n, o[2], rows, o[0], at)
             rings[c].append(ring)
             ring.start()
     for r in rings:
         r[2].forward()
+    for r in rings:
+        r[2].sides()
     for c, (rows, o) in enumerate(COLOURS):
         at = rings[c][1].far()
-        share(at, o[0], rows)
         ring = Ring(c * N_RING + 5, o[2], rows, o[0], at)
         rings[c].append(ring)
         ring.start()
     for n in (3, 4):
         for r in rings:
             r[n].forward()
+        for r in rings:
+            r[n].sides()
     corr_forward()
-    for c, (rows, o) in enumerate(COLOURS):
-        for at in rings[c][2].sides():
-            share(at, o[0], rows)
-        share(rings[c][2].far(), o[0], rows)
+    for r in rings:
+        r[2].far()
     for r in rings:
         r[5].forward()
+    for r in rings:
+        r[5].sides()
     for n in (3, 4, 5):
-        for c, (rows, o) in enumerate(COLOURS):
-            for at in rings[c][n].sides():
-                share(at, o[0], rows)
-            share(rings[c][n].far(), o[0], rows)
+        for r in rings:
+            r[n].far()
 
     for c in pending:
         c.wait_send()
     to_partner.wait_send()
     other = kall.at[me["y"], partner["h"], me["x"], me["z"]]
-    copy(other, other, 54, (dsend, drecv), partner).wait_recv()
+    copy(other, other, 108, (dsend, drecv), partner).wait_recv()
     for n, (c, at, whole, rows) in enumerate(shared):
         c.wait_send()
         r = region(at, whole, rows)
@@ -315,8 +339,8 @@
             dma,
             dma((108,)),
             dma((108,)),
-            dma((55,)),
-            dma((55,)),
+            dma((109,)),
+            dma((109,)),
             dma((6,)),
             dma((6,)),
             dma((8,)),
@@ -416,26 +440,27 @@
     hsem, rsend, rrecv, psend, precv, asend, arecv, gsend, grecv,
 ):
     row, col = lax.axis_index("row"), lax.axis_index("col")
-    to_row, to_col = 2 * col + lax.div(row, 8), lax.rem(row, 8)
-    own = 8 * row + col
-    from_row, from_col = lax.rem(own, 16), lax.div(own, 16)
-    moves = jnp.logical_or(to_row != row, to_col != col)
+    x, z, y, h = lax.div(row, 4), lax.rem(row, 4), lax.div(col, 2), lax.rem(col, 2)
+
+    def block_of(at_row):
+        to_y = lax.rem(2 * y + 6 - lax.div(at_row, 4), 4)
+        turn = lax.rem(lax.rem(at_row, 4) + 4 - 2 * h, 4)
+        return 8 * lax.rem(lax.div(turn + 1, 2), 2) + 2 * to_y + lax.div(turn, 2)
+
+    mine = block_of(row)
+    to_row, to_col = 2 * col + lax.div(mine, 8), lax.rem(mine, 8)
+    low = lax.rem(z, 2)
+    from_z = lax.rem(2 * lax.div(z, 2) + low + h * (2 * low - 1) + 4, 4)
+    from_row, from_col = 4 * lax.rem(2 * x + 6 - y, 4) + from_z, 2 * x + lax.div(z, 2)
 
     barrier = pltpu.get_barrier_semaphore()
     for by in range(1, 16):
         pl.semaphore_signal(barrier, inc=1, device_id=(lax.rem(row + by, 16), col), device_id_type=MESH)
     for by in range(1, 8):
         pl.semaphore_signal(barrier, inc=1, device_id=(row, lax.rem(col + by, 8)), device_id_type=MESH)
-
-    @pl.when(moves)
-    def _():
-        pl.semaphore_signal(barrier, inc=1, device_id=(to_row, to_col), device_id_type=MESH)
-        pl.semaphore_signal(barrier, inc=1, device_id=(from_row, from_col), device_id_type=MESH)
-        pl.semaphore_wait(barrier, 24)
-
-    @pl.when(jnp.logical_not(moves))
-    def _():
-        pl.semaphore_wait(barrier, 22)
+    pl.semaphore_signal(barrier, inc=1, device_id=(to_row, to_col), device_id_type=MESH)
+    pl.semaphore_signal(barrier, inc=1, device_id=(from_row, from_col), device_id_type=MESH)
+    pl.semaphore_wait(barrier, 24)
 
     fetch = pltpu.make_async_copy(ham, hamv, hsem)
     fetch.start()
@@ -449,29 +474,28 @@
     inverse = 1.0 / energy[...]
     for step in range(STEPS):
         last = step == STEPS - 1
-        outgoing = part if step == 0 else parts
         sent = []
         for by in range(1, 16):
             to = lax.rem(row + by, 16)
             if step > 0:
-                columns = pl.ds(pl.multiple_of(to * 256, 256), 256)
+                columns = pl.ds(pl.multiple_of(block_of(to) * 256, 256), 256)
                 total = jnp.zeros((64, 256), F32)
                 for k in range(8):
                     total += jnp.dot(curb[k], hamv[pl.ds(k * 256, 256), columns], preferred_element_type=F32)
                 parts[by] = total.astype(BF16)
                 src = parts.at[by]
             else:
-                src = part.at[to]
+                src = part.at[block_of(to)]
             c = remote(src, rsbuf.at[step, by], rsend.at[step, by], rrecv.at[step, by], (to, col))
             c.start()
             sent.append(c)
         if step > 0:
-            columns = pl.ds(pl.multiple_of(row * 256, 256), 256)
+            columns = pl.ds(pl.multiple_of(mine * 256, 256), 256)
             total = jnp.zeros((64, 256), F32)
             for k in range(8):
                 total += jnp.dot(curb[k], hamv[pl.ds(k * 256, 256), columns], preferred_element_type=F32)
         else:
-            total = part[row].astype(F32)
+            total = part[mine].astype(F32)
         for by in range(1, 16):
             remote(
                 rsbuf.at[step, by], rsbuf.at[step, by], rsend.at[step, by], rrecv.at[step, by], (row, col)
@@ -479,19 +503,10 @@
             total += rsbuf[step, by].astype(F32)
         image[step] = total.astype(BF16)
 
-        @pl.when(moves)
-        def _():
-            c = remote(image.at[step], agbuf.at[step, to_col], psend.at[step], precv.at[step], (to_row, to_col))
-            c.start()
-            c.wait_send()
-            remote(
-                agbuf.at[step, col], agbuf.at[step, col], psend.at[step], precv.at[step], (row, col)
-            ).wait_recv()
-
-        @pl.when(jnp.logical_not(moves))
-        def _():
-            agbuf[step, col] = image[step]
-
+        c = remote(image.at[step], agbuf.at[step, to_col], psend.at[step], precv.at[step], (to_row, to_col))
+        c.start()
+        sent.append(c)
+        remote(agbuf.at[step, col], agbuf.at[step, col], psend.at[step], precv.at[step], (row, col)).wait_recv()
         for by in range(1, 8):
             to = lax.rem(col + by, 8)
             c = remote(

time: 190 us -> 182 us (0.958)
  Pallas kernels: 185 us -> 178 us
    pallas_call x1, Pallas kernels: 93.1 us -> 86.4 us  [gathered(): pl.pallas_call(gather_kernel, out_shape=(jax.ShapeDtypeStruct((4, 2, 4, 4...]
where the time goes in v3:
time: 182 us
  Pallas kernels  178 us (98%)
  local copies, waits for them, and re-layouts  2.29 us (1%)
    pallas_call x1, Pallas kernels, gathered(): pl.pallas_call(gather_kernel, out_shape=(jax.ShapeDtypeStruct((4, 2, 4, 4...  86.4 us
    pallas_call x1, Pallas kernels, powered(): pl.pallas_call(power_kernel, out_shape=(jax.ShapeDtypeStruct((64, 256), F...  66.4 us
    pallas_call x1, Pallas kernels, tiled(): pl.pallas_call(tile_kernel, grid_spec=grid_spec, out_shape=(jax.ShapeDtyp...  25.1 us

profile of v3, /device:TPU:0, one launch (start us, length us, event | category | flops | bytes accessed | tf_op | source)
XLA Modules:
  0.0 181.6 jit_solution(9715485597205042415)
XLA Ops:
  0.6 86.4 %gather.1 = (bf16[4,2,4,4,512,256]{5,4,3,2,1,0:T(8,128)(2,1)}, bf16[8,256,256]{2,1,0:T(8,128)(2,1)}, f32[8,64,256]{2,1,0:T(8,128)}) custom-call(bf16[512,256]{1,0:T(8,128)(2,1)} %bitcast.15, bf16[16,256,256]{2,1,0:T(8,128)(2,1)} %refs_9_.1, f32[64,256]{1,0:T(8,128)} %bitcast.16), custom_call_target="tpu_custom_call" | custom-call | tf_op jit(solution)/shard_map/gather/pallas_call | solution.py:329
  87.0 0.6 pad_add_fusion.pos
  87.7 0.0 copy-start.2
  87.7 0.0 copy-start
  87.7 25.1 %tiles.1 = (bf16[2048,4096]{1,0:T(8,128)(2,1)}, bf16[16,64,256]{2,1,0:T(8,128)(2,1)}) custom-call(s32[128]{0:T(128)} %co.1, s32[2]{0:T(128)} %pad_add_fusion.pos, bf16[8,16,2,256,256]{4,3,2,1,0:T(8,128)(2,1)} %bitcast.7, bf16[8,16,2,256,256]{4,3,2,1,0:T(8,128)(2,1)} %bitcast.8, bf16[8,16,2,256,256]{4,3,2,1,0:T(8,128)(2,1)} %bitcast.9, ...), custom_call_target="tpu_custom_call" | custom-call | tf_op jit(solution)/shard_map/tiles/pallas_call | solution.py:399
  112.8 0.0 copy-done.2
  112.8 0.0 copy-done
  112.9 0.0 copy-start.1
  112.9 1.0 copy-done.1
  113.9 66.4 %power.1 = (f32[64,256]{1,0:T(8,128)S(1)}, f32[64,64]{1,0:T(8,128)S(1)}) custom-call(bf16[16,64,256]{2,1,0:T(8,128)(2,1)S(1)} %copy-done.1, bf16[2048,4096]{1,0:T(8,128)(2,1)} %get-tuple-element.20.ham, f32[8,256]{1,0:T(8,128)S(1)} %reshape.17.energy, f32[8,64,256]{2,1,0:T(8,128)S(1)} %copy-done), custom_call_target="tpu_custom_call" | custom-call | tf_op jit(solution)/shard_map/power/pallas_call | solution.py:564
  180.4 0.6 copy.10
  181.0 0.6 copy.11
  (1 shorter events, 0.0 us)
Async XLA Ops:
  87.7 25.2 %copy-start.2 = (f32[2048]{0:T(1024)S(1)}, f32[2048]{0:T(1024)}, u32[]{:S(2)}) copy-start(f32[2048]{0:T(1024)} %param.8) | copy-start | bytes 24580
  87.7 25.2 %copy-start = (f32[8,64,256]{2,1,0:T(8,128)S(1)}, f32[8,64,256]{2,1,0:T(8,128)}, u32[]{:S(2)}) copy-start(f32[8,64,256]{2,1,0:T(8,128)} %get-tuple-element.12.refs_10_.seg) | copy-start | bytes 1572868
  112.9 1.0 copy-start.1

commit v4 on v3

--- a/solution.py
+++ b/solution.py
@@ -18,8 +18,8 @@
 
 COLOURS = (
     ((0, 192), "xyz"),
-    ((192, 176), "yzx"),
-    ((368, 144), "zxy"),
+    ((192, 192), "yzx"),
+    ((384, 128), "zxy"),
 )
 N_RING = 6
 

time: 182 us -> 183 us (level)
  no operation moved by 1% of the time
where the time goes in v4:
time: 183 us
  Pallas kernels  179 us (98%)
  local copies, waits for them, and re-layouts  2.29 us (1%)
    pallas_call x1, Pallas kernels, gathered(): pl.pallas_call(gather_kernel, out_shape=(jax.ShapeDtypeStruct((4, 2, 4, 4...  87.4 us
    pallas_call x1, Pallas kernels, powered(): pl.pallas_call(power_kernel, out_shape=(jax.ShapeDtypeStruct((64, 256), F...  66.4 us
    pallas_call x1, Pallas kernels, tiled(): pl.pallas_call(tile_kernel, grid_spec=grid_spec, out_shape=(jax.ShapeDtyp...  25.1 us

profile of v4, /device:TPU:0, one launch (start us, length us, event | category | flops | bytes accessed | tf_op | source)
XLA Modules:
  0.0 182.6 jit_solution(3085125529453424255)
XLA Ops:
  0.6 87.4 %gather.1 = (bf16[4,2,4,4,512,256]{5,4,3,2,1,0:T(8,128)(2,1)}, bf16[8,256,256]{2,1,0:T(8,128)(2,1)}, f32[8,64,256]{2,1,0:T(8,128)}) custom-call(bf16[512,256]{1,0:T(8,128)(2,1)} %bitcast.15, bf16[16,256,256]{2,1,0:T(8,128)(2,1)} %refs_9_.1, f32[64,256]{1,0:T(8,128)} %bitcast.16), custom_call_target="tpu_custom_call" | custom-call | tf_op jit(solution)/shard_map/gather/pallas_call | solution.py:329
  88.1 0.6 pad_add_fusion.pos
  88.7 0.0 copy-start.2
  88.7 0.0 copy-start
  88.7 25.1 %tiles.1 = (bf16[2048,4096]{1,0:T(8,128)(2,1)}, bf16[16,64,256]{2,1,0:T(8,128)(2,1)}) custom-call(s32[128]{0:T(128)} %co.1, s32[2]{0:T(128)} %pad_add_fusion.pos, bf16[8,16,2,256,256]{4,3,2,1,0:T(8,128)(2,1)} %bitcast.7, bf16[8,16,2,256,256]{4,3,2,1,0:T(8,128)(2,1)} %bitcast.8, bf16[8,16,2,256,256]{4,3,2,1,0:T(8,128)(2,1)} %bitcast.9, ...), custom_call_target="tpu_custom_call" | custom-call | tf_op jit(solution)/shard_map/tiles/pallas_call | solution.py:399
  113.9 0.0 copy-done.2
  113.9 0.0 copy-done
  113.9 0.0 copy-start.1
  113.9 1.0 copy-done.1
  115.0 66.4 %power.1 = (f32[64,256]{1,0:T(8,128)S(1)}, f32[64,64]{1,0:T(8,128)S(1)}) custom-call(bf16[16,64,256]{2,1,0:T(8,128)(2,1)S(1)} %copy-done.1, bf16[2048,4096]{1,0:T(8,128)(2,1)} %get-tuple-element.20.ham, f32[8,256]{1,0:T(8,128)S(1)} %reshape.17.energy, f32[8,64,256]{2,1,0:T(8,128)S(1)} %copy-done), custom_call_target="tpu_custom_call" | custom-call | tf_op jit(solution)/shard_map/power/pallas_call | solution.py:564
  181.4 0.6 copy.10
  182.0 0.6 copy.11
  (1 shorter events, 0.0 us)
Async XLA Ops:
  88.7 25.2 %copy-start.2 = (f32[2048]{0:T(1024)S(1)}, f32[2048]{0:T(1024)}, u32[]{:S(2)}) copy-start(f32[2048]{0:T(1024)} %param.8) | copy-start | bytes 24580
  88.7 25.2 %copy-start = (f32[8,64,256]{2,1,0:T(8,128)S(1)}, f32[8,64,256]{2,1,0:T(8,128)}, u32[]{:S(2)}) copy-start(f32[8,64,256]{2,1,0:T(8,128)} %get-tuple-element.12.refs_10_.seg) | copy-start | bytes 1572868
  113.9 1.0 copy-start.1
